TPU v7x, 32 devices: a whole 2x2x4 slice. The times are simulated.
32 devices in a mesh: dp: 2 (over y), mp: 16 (over z, x, core).
Axes of the slice: x: 2, y: 2, z: 4, core: 2. Of those that a mesh axis runs over, the one named last changes fastest.
Arguments:
- features: bfloat16 [32, 1280, 1024], P('dp', 'mp'), may hold values from -6 to 6
- conv_weight: bfloat16 [1280, 1280], P('mp'), may hold values from -0.15625 to 0.15625
- norm_gain: float32 [1280], replicated, may hold values from 0.25 to 1.75
- norm_bias: float32 [1280], replicated, may hold values from -3 to 3
- logit_vector: float32 [1280], replicated, may hold values from -0.625 to 0.625
- labels: int32 [32], P(('dp', 'mp')), may hold values 0 or 1
Outputs:
- grad_features: float32 [32, 1280, 1024], P('dp', 'mp')
- grad_weight: float32 [1280, 1280], P('mp')
- head_grads: float32 [3, 1280], replicated
- loss: float32 [], replicated
All inputs are finite; a program needn't handle non-finite values. No bound on the sum of `labels` on one device may be relied on, other than what follows from the above.
Results may differ from a plain program's by a relative error of at most 0.0029.
Values may be sent and summed in bfloat16 or wider, within the bound.
No kernel may reach another device: no remote copies, remote signals or barrier semaphores. Data moves between devices by JAX's collectives and lax.ppermute only.
A program may use at most 128 MiB of HBM per device.

v0:
```python
import jax
import jax.numpy as jnp
from jax import lax
from jax.sharding import PartitionSpec as P

GROUPS = 32
norm_eps = 1e-05


def head_total(pre, norm_gain, norm_bias, logit_vector, signs):
    images, channels, cell_count = pre.shape
    grouped = pre.reshape(images, GROUPS, channels // GROUPS, cell_count)
    center = jnp.mean(grouped, axis=(2, 3), keepdims=True)
    spread = jnp.mean((grouped - center) ** 2, axis=(2, 3), keepdims=True)
    normed = ((grouped - center) * lax.rsqrt(spread + norm_eps)).reshape(
        images, channels, cell_count
    )
    normed = normed * norm_gain[:, None] + norm_bias[:, None]
    hidden = jax.nn.silu(normed)
    logits = (
        jnp.einsum("c,ncs->n", logit_vector, hidden, precision=lax.Precision.HIGHEST) / cell_count
    )
    margin = jnp.maximum(1.0 - signs * logits, 0.0)
    return jnp.sum(margin * margin)


def shards(features, conv_weight, norm_gain, norm_bias, logit_vector, labels):
    signs = 2.0 * labels.astype(jnp.float32) - 1.0
    weight_full = lax.all_gather(conv_weight, "mp", axis=0, tiled=True)
    image_block = lax.all_to_all(features, "mp", split_axis=0, concat_axis=1, tiled=True)
    pre = jnp.einsum("io,nis->nos", weight_full, image_block, preferred_element_type=jnp.float32)
    total, pull = jax.vjp(
        lambda p, g, b, h: head_total(p, g, b, h, signs), pre, norm_gain, norm_bias, logit_vector
    )
    grad_pre, grad_gain, grad_bias, grad_vec = pull(jnp.ones((), jnp.float32))
    grad_pre = grad_pre.astype(jnp.bfloat16)
    grad_image = jnp.einsum(
        "io,nos->nis", weight_full, grad_pre, preferred_element_type=jnp.float32
    )
    grad_features = lax.all_to_all(grad_image, "mp", split_axis=1, concat_axis=0, tiled=True)
    weight_term = jnp.einsum(
        "nis,nos->io", image_block, grad_pre, preferred_element_type=jnp.float32
    )
    summed = lax.psum(weight_term, "dp")
    grad_weight = lax.psum_scatter(summed, "mp", scatter_dimension=0, tiled=True)
    total_sum, head_grads = lax.psum(
        (total, jnp.stack([grad_gain, grad_bias, grad_vec])), ("dp", "mp")
    )
    image_total = pre.shape[0] * lax.axis_size("dp") * lax.axis_size("mp")
    loss = total_sum / image_total
    return (grad_features, grad_weight, head_grads, loss)


def solution(mesh):
    return jax.shard_map(
        shards,
        mesh=mesh,
        in_specs=(P("dp", "mp", None), P("mp", None), P(), P(), P(), P(("dp", "mp"))),
        out_specs=(P("dp", "mp", None), P("mp", None), P(), P()),
        check_vma=False,
    )
```

profile of v0, /device:TPU:12, one launch (start us, length us, event | category | flops | bytes accessed | tf_op | source)
XLA Modules:
  0.0 369.9 jit_solution(1314709763259043762)
XLA Ops:
  7.2 0.7 all-gather.2.cloned.1.call-update
  7.9 6.3 %all-to-all-start = ((bf16[16,80,1024]{2,1,0:T(8,128)(2,1)}), bf16[16,80,1024]{2,1,0:T(8,128)(2,1)S(1)}, u32[]{:S(2)}, u32[]{:S(2)}) async-start(bf16[16,80,1024]{2,1,0:T(8,128)(2,1)} %param.6), calls=%async_computation | async-start | bytes 5242880 | tf_op jit(solution)/shard_map/all_to_all | solution.py:30
  14.9 76.1 %all-to-all-done = bf16[16,80,1024]{2,1,0:T(8,128)(2,1)S(1)} async-done(((bf16[16,80,1024]{2,1,0:T(8,128)(2,1)}), bf16[16,80,1024]{2,1,0:T(8,128)(2,1)S(1)}, u32[]{:S(2)}, u32[]{:S(2)}) %all-to-all-start) | async-done | bytes 2621472 | tf_op jit(solution)/shard_map/all_to_all | solution.py:30
  91.0 7.3 %fusion.10 = (f32[1280]{0:T(1024)S(1)}, f32[1024,1280]{1,0:T(8,128)}) fusion(bf16[1280,1024]{1,0:T(8,128)(2,1)S(1)} %bitcast.86, bf16[1280,1280]{1,0:T(8,128)(2,1)} %all-gather.2.cloned.1.call-done), kind=kOutput, calls=%fused_computation.30 | convolution fusion | flops 3356752640 | bytes 11146240 | tf_op jit(solution)/shard_map/io,nis->nos/dot_general | solution.py:31
  98.4 0.1 reduce_sum.139
  98.6 0.1 sub.53
  98.7 3.1 fusion.2
  101.8 0.1 reduce_sum.141
  101.9 0.1 reduce_sum.142
  102.1 0.1 mul.156
  102.2 4.2 %multiply_reduce_fusion.1 = f32[1280]{0:T(1024)S(1)} fusion(f32[1024,1280]{1,0:T(8,128)} %get-tuple-element.27, f32[1280]{0:T(1024)S(1)} %copy-done, f32[1280]{0:T(1024)S(1)} %copy-done.1, f32[1280]{0:T(1024)S(1)} %mul.156, f32[1280]{0:T(1024)S(1)} %sub.53), kind=kLoop, calls=%fused_computation.13 | loop fusion | flops 11795200 | bytes 5268480 | tf_op jit(solution)/shard_map/jvp(c,ncs->n)/reduce_sum | solution.py:21
  106.4 0.6 multiply_reduce_fusion.3
  107.7 5.7 %multiply_reduce_fusion = (f32[1280]{0:T(1024)S(1)}, f32[1280]{0:T(1024)S(1)}, f32[1280]{0:T(1024)S(1)}, f32[1280]{0:T(1024)S(1)}) fusion(f32[1024,1280]{1,0:T(8,128)} %get-tuple-element.27, f32[1280]{0:T(1024)S(1)} %mul.156, f32[1280]{0:T(1024)S(1)} %sub.53, f32[1280]{0:T(1024)S(1)} %copy-done, f32[1280]{0:T(1024)S(1)} %copy-done.1, ...), kind=kLoop, calls=%fused_computation.11 | loop fusion | flops 27520000 | bytes 5288960 | tf_op jit(solution)/shard_map/transpose(jvp())/reduce_sum | solution.py:18
  113.4 0.1 reduce_sum.148
  113.5 0.1 reduce_sum.149
  113.6 0.1 reduce_sum.145
  113.7 0.1 reduce_sum.146
  113.9 0.1 mul.178
  114.0 3.1 fusion.4
  117.1 0.1 reduce_sum.151
  117.2 0.1 reduce_sum.152
  117.4 0.1 broadcast_in_dim.10
  117.5 11.6 %convolution_bitcast_fusion = f32[1280,1280]{0,1:T(8,128)} fusion(bf16[1280,1024]{1,0:T(8,128)(2,1)S(1)} %bitcast.87, f32[1024,1280]{1,0:T(8,128)} %get-tuple-element.27, f32[1280]{0:T(1024)S(1)} %broadcast_in_dim.10, f32[1280]{0:T(1024)S(1)} %mul.178, f32[1280]{0:T(1024)S(1)} %copy-done.1, f32[1280]{0:T(1024)S(1)} %mul.156, f32[1280]{0:T(1024)S(1)} %sub.53, ...), kind=kOutput, calls=%fused_computation | convolution fusion | flops 3380346880 | bytes 14453760 | tf_op jit(solution)/shard_map/nis,nos->io/dot_general | solution.py:41
  129.1 8.2 %copy.20 = f32[1280,1280]{1,0:T(8,128)} copy(f32[1280,1280]{0,1:T(8,128)} %convolution_bitcast_fusion) | data formatting | bytes 13107200
  137.3 12.1 %convolution_bitcast_fusion.1 = f32[1,1280,1024]{1,2,0:T(8,128)} fusion(bf16[1280,1280]{1,0:T(8,128)(2,1)} %all-gather.2.cloned.1.call-done, f32[1024,1280]{1,0:T(8,128)} %get-tuple-element.27, f32[1280]{0:T(1024)S(1)} %broadcast_in_dim.10, f32[1280]{0:T(1024)S(1)} %mul.178, f32[1280]{0:T(1024)S(1)} %copy-done.1, f32[1280]{0:T(1024)S(1)} %mul.156, ...), kind=kOutput, calls=%fused_computation.18 | convolution fusion | flops 3380346880 | bytes 13798400 | tf_op jit(solution)/shard_map/io,nos->nis/dot_general | solution.py:37
  149.4 11.9 %copy.16 = f32[1,1280,1024]{2,0,1:T(1,128)} copy(f32[1,1280,1024]{1,2,0:T(8,128)} %convolution_bitcast_fusion.1) | data formatting | bytes 10485760 | tf_op jit(solution)/shard_map/io,nos->nis/transpose | solution.py:37
  161.3 6.4 %all-to-all-start.1 = ((f32[1,1280,1024]{2,0,1:T(1,128)}), f32[1,1280,1024]{2,0,1:T(1,128)}, u32[]{:S(2)}, u32[]{:S(2)}) async-start(f32[1,1280,1024]{2,0,1:T(1,128)} %copy.16), calls=%async_computation.1 | async-start | bytes 10485760 | tf_op jit(solution)/shard_map/all_to_all | solution.py:40
  167.7 133.2 %reduce-scatter.4.cloned.1.call-done = f32[80,1280]{1,0:T(8,128)} async-done(((f32[1280,1280]{1,0:T(8,128)}), f32[80,1280]{1,0:T(8,128)}) %reduce-scatter.4.cloned.1.call-update) | async-done | bytes 409616
  300.9 2.1 copy.21
  303.1 50.3 %all-reduce = (f32[3,1280]{1,0:T(4,128)}, f32[]{:T(128)}) all-reduce(f32[3,1280]{1,0:T(4,128)S(1)} %pad_maximum_fusion, f32[]{:T(128)} %bitcast.9), channel_id=1, replica_groups=mesh['dp'=2,'mp'=16] {'dp','mp'}, use_global_device_ids=true, to_apply=%region_15.16 | all-reduce | flops 3841 | bytes 30728 | tf_op jit(solution)/shard_map/psum | solution.py:46
  354.0 6.1 %copy.22 = f32[1,1280,1024]{2,1,0:T(8,128)} copy(f32[1,1280,1024]{2,0,1:T(1,128)} %all-to-all-done.1) | data formatting | bytes 10485760
  360.2 2.1 copy.17
  (29 shorter events, 0.6 us)
Async XLA Ops:
  7.2 83.9 %all-gather.2.cloned.1.call-start = ((), (), s32[]{:S(2)}) async-start(), calls=%async_computation.3 | async-start | bytes 3481600 | tf_op jit(solution)/shard_map/all_gather | solution.py:29
  7.9 83.1 %all-to-all-start = ((bf16[16,80,1024]{2,1,0:T(8,128)(2,1)}), bf16[16,80,1024]{2,1,0:T(8,128)(2,1)S(1)}, u32[]{:S(2)}, u32[]{:S(2)}) async-start(bf16[16,80,1024]{2,1,0:T(8,128)(2,1)} %param.6), calls=%async_computation | async-start | bytes 5242880 | tf_op jit(solution)/shard_map/all_to_all | solution.py:30
  14.2 286.7 %reduce-scatter.4.cloned.1.call-start = ((), (), s32[]{:S(2)}) async-start(), calls=%async_computation.5 | async-start | bytes 6963200
  98.3 3.9 %copy-start = (f32[1280]{0:T(1024)S(1)}, f32[1280]{0:T(1024)}, u32[]{:S(2)}) copy-start(f32[1280]{0:T(1024)} %param.9) | copy-start | bytes 15364
  98.3 3.9 %copy-start.1 = (f32[1280]{0:T(1024)S(1)}, f32[1280]{0:T(1024)}, u32[]{:S(2)}) copy-start(f32[1280]{0:T(1024)} %param.8) | copy-start | bytes 15364
  98.7 7.7 %copy-start.2 = (f32[1280]{0:T(1024)S(1)}, f32[1280]{0:T(1024)}, u32[]{:S(2)}) copy-start(f32[1280]{0:T(1024)} %param.10) | copy-start | bytes 15364
  161.3 192.7 %all-to-all-start.1 = ((f32[1,1280,1024]{2,0,1:T(1,128)}), f32[1,1280,1024]{2,0,1:T(1,128)}, u32[]{:S(2)}, u32[]{:S(2)}) async-start(f32[1,1280,1024]{2,0,1:T(1,128)} %copy.16), calls=%async_computation.1 | async-start | bytes 10485760 | tf_op jit(solution)/shard_map/all_to_all | solution.py:40
  167.7 192.5 %all-reduce.3.cloned.1.call-start = ((), (), s32[]{:S(2)}) async-start(), calls=%async_computation.4 | async-start | bytes 1310720 | tf_op jit(solution)/shard_map/psum | solution.py:44
Sparse Core Ops, SparseCore 0:
  10.3 75.0 all-gather.1
  137.4 163.3 reduce-scatter.3
  303.2 30.7 all-reduce.2
where the time goes:
time: 371 us; the launch traced here: 370 us
  waiting for transfers between devices  210 us (57%)
  blocking collectives  50.3 us (14%)
  local copies, waits for them, and re-layouts  31.4 us (8%)
  matrix products  31.1 us (8%)
  other arithmetic  17.3 us (5%)
  between operations  17 us (5%)
  starting transfers between devices  12.8 us (3%)
    unnamed x4, waiting for transfers between devices  134 us
    all_to_all x1, waiting for transfers between devices, shards(): lax.all_to_all(features, 'mp', split_axis=0, concat_axis=1, tiled=True)  76.1 us
    psum x1, blocking collectives, shards(): lax.psum((total, jnp.stack([grad_gain, grad_bias, grad_vec])), ('dp', 'mp'))  50.3 us
    unnamed x10, local copies, waits for them, and re-layouts  18.4 us
    dot_general x1, matrix products, shards(): jnp.einsum('io,nos->nis', weight_full, grad_pre, preferred_element_type=j...  12.1 us
    transpose x1, local copies, waits for them, and re-layouts, shards(): jnp.einsum('io,nos->nis', weight_full, grad_pre, preferred_element_type=j...  11.9 us
    dot_general x1, matrix products, shards(): jnp.einsum('nis,nos->io', image_block, grad_pre, preferred_element_type=j...  11.6 us
  transfers between devices with their start and end apart: 5, of which 2 were waited for; matrix products, arithmetic and copies ran while one was open for 9% of the time, Pallas kernels for 0%

commit v1 on v0

--- a/solution.py
+++ b/solution.py
@@ -5,6 +5,11 @@
 
 GROUPS = 32
 norm_eps = 1e-05
+
+
+def axis_by_axis(value, inner_axis, outer_axis):
+    partial = lax.psum(value, inner_axis)
+    return lax.psum(partial, outer_axis)
 
 
 def head_total(pre, norm_gain, norm_bias, logit_vector, signs):
@@ -43,8 +48,8 @@
     )
     summed = lax.psum(weight_term, "dp")
     grad_weight = lax.psum_scatter(summed, "mp", scatter_dimension=0, tiled=True)
-    total_sum, head_grads = lax.psum(
-        (total, jnp.stack([grad_gain, grad_bias, grad_vec])), ("dp", "mp")
+    total_sum, head_grads = axis_by_axis(
+        (total, jnp.stack([grad_gain, grad_bias, grad_vec])), "mp", "dp"
     )
     image_total = pre.shape[0] * lax.axis_size("dp") * lax.axis_size("mp")
     loss = total_sum / image_total

time: 371 us -> 390 us (1.051); the launches traced: 370 us -> 383 us
  blocking collectives: 50.3 us -> 63.5 us
    psum x1 -> x2, blocking collectives: 50.3 us -> 63.5 us  [the longest x1 55.1 us: axis_by_axis(): partial = lax.psum(value, inner_axis)]
  transfers between devices with their start and end apart: 5 -> 5, of which waited for: 2 -> 2; matrix products, arithmetic and copies ran while one was open for 9% -> 8% of each run, Pallas kernels for 0% -> 0%
where the time goes in v1:
time: 390 us; the launch traced here: 383 us
  waiting for transfers between devices  210 us (54%)
  blocking collectives  63.5 us (16%)
  local copies, waits for them, and re-layouts  31.4 us (8%)
  matrix products  31.1 us (8%)
  other arithmetic  17.3 us (4%)
  between operations  17 us (4%)
  starting transfers between devices  12.8 us (3%)
    unnamed x4, waiting for transfers between devices  134 us
    all_to_all x1, waiting for transfers between devices, shards(): lax.all_to_all(features, 'mp', split_axis=0, concat_axis=1, tiled=True)  76.1 us
    psum x1, blocking collectives, axis_by_axis(): partial = lax.psum(value, inner_axis)  55.1 us
    unnamed x10, local copies, waits for them, and re-layouts  18.4 us
    dot_general x1, matrix products, shards(): jnp.einsum('io,nos->nis', weight_full, grad_pre, preferred_element_type=j...  12.1 us
    transpose x1, local copies, waits for them, and re-layouts, shards(): jnp.einsum('io,nos->nis', weight_full, grad_pre, preferred_element_type=j...  11.9 us
    dot_general x1, matrix products, shards(): jnp.einsum('nis,nos->io', image_block, grad_pre, preferred_element_type=j...  11.6 us
    psum x1, blocking collectives, axis_by_axis(): return lax.psum(partial, outer_axis)  8.42 us
  transfers between devices with their start and end apart: 5, of which 2 were waited for; matrix products, arithmetic and copies ran while one was open for 8% of the time, Pallas kernels for 0%

profile of v1, /device:TPU:12, one launch (start us, length us, event | category | flops | bytes accessed | tf_op | source)
XLA Modules:
  0.0 383.1 jit_solution(6290655433045862350)
XLA Ops:
  7.2 0.7 all-gather.2.cloned.1.call-update
  7.9 6.3 %all-to-all-start = ((bf16[16,80,1024]{2,1,0:T(8,128)(2,1)}), bf16[16,80,1024]{2,1,0:T(8,128)(2,1)S(1)}, u32[]{:S(2)}, u32[]{:S(2)}) async-start(bf16[16,80,1024]{2,1,0:T(8,128)(2,1)} %param.6), calls=%async_computation | async-start | bytes 5242880 | tf_op jit(solution)/shard_map/all_to_all | solution.py:35
  14.9 76.1 %all-to-all-done = bf16[16,80,1024]{2,1,0:T(8,128)(2,1)S(1)} async-done(((bf16[16,80,1024]{2,1,0:T(8,128)(2,1)}), bf16[16,80,1024]{2,1,0:T(8,128)(2,1)S(1)}, u32[]{:S(2)}, u32[]{:S(2)}) %all-to-all-start) | async-done | bytes 2621472 | tf_op jit(solution)/shard_map/all_to_all | solution.py:35
  91.0 7.3 %fusion.10 = (f32[1280]{0:T(1024)S(1)}, f32[1024,1280]{1,0:T(8,128)}) fusion(bf16[1280,1024]{1,0:T(8,128)(2,1)S(1)} %bitcast.86, bf16[1280,1280]{1,0:T(8,128)(2,1)} %all-gather.2.cloned.1.call-done), kind=kOutput, calls=%fused_computation.30 | convolution fusion | flops 3356752640 | bytes 11146240 | tf_op jit(solution)/shard_map/io,nis->nos/dot_general | solution.py:36
  98.4 0.1 reduce_sum.139
  98.6 0.1 sub.53
  98.7 3.1 fusion.2
  101.8 0.1 reduce_sum.141
  101.9 0.1 reduce_sum.142
  102.1 0.1 mul.156
  102.2 4.2 %multiply_reduce_fusion.1 = f32[1280]{0:T(1024)S(1)} fusion(f32[1024,1280]{1,0:T(8,128)} %get-tuple-element.29, f32[1280]{0:T(1024)S(1)} %copy-done, f32[1280]{0:T(1024)S(1)} %copy-done.1, f32[1280]{0:T(1024)S(1)} %mul.156, f32[1280]{0:T(1024)S(1)} %sub.53), kind=kLoop, calls=%fused_computation.13 | loop fusion | flops 11795200 | bytes 5268480 | tf_op jit(solution)/shard_map/jvp(c,ncs->n)/reduce_sum | solution.py:26
  106.4 0.6 multiply_reduce_fusion.3
  107.7 5.7 %multiply_reduce_fusion = (f32[1280]{0:T(1024)S(1)}, f32[1280]{0:T(1024)S(1)}, f32[1280]{0:T(1024)S(1)}, f32[1280]{0:T(1024)S(1)}) fusion(f32[1024,1280]{1,0:T(8,128)} %get-tuple-element.29, f32[1280]{0:T(1024)S(1)} %mul.156, f32[1280]{0:T(1024)S(1)} %sub.53, f32[1280]{0:T(1024)S(1)} %copy-done, f32[1280]{0:T(1024)S(1)} %copy-done.1, ...), kind=kLoop, calls=%fused_computation.11 | loop fusion | flops 27520000 | bytes 5288960 | tf_op jit(solution)/shard_map/transpose(jvp())/reduce_sum | solution.py:23
  113.5 0.1 reduce_sum.149
  113.6 0.1 reduce_sum.145
  113.7 0.1 reduce_sum.146
  113.9 0.1 mul.178
  114.0 3.1 fusion.4
  117.1 0.1 reduce_sum.151
  117.2 0.1 reduce_sum.152
  117.4 0.1 broadcast_in_dim.10
  117.5 11.6 %convolution_bitcast_fusion = f32[1280,1280]{0,1:T(8,128)} fusion(bf16[1280,1024]{1,0:T(8,128)(2,1)S(1)} %bitcast.87, f32[1024,1280]{1,0:T(8,128)} %get-tuple-element.29, f32[1280]{0:T(1024)S(1)} %broadcast_in_dim.10, f32[1280]{0:T(1024)S(1)} %mul.178, f32[1280]{0:T(1024)S(1)} %copy-done.1, f32[1280]{0:T(1024)S(1)} %mul.156, f32[1280]{0:T(1024)S(1)} %sub.53, ...), kind=kOutput, calls=%fused_computation | convolution fusion | flops 3380346880 | bytes 14453760 | tf_op jit(solution)/shard_map/nis,nos->io/dot_general | solution.py:46
  129.1 8.2 %copy.20 = f32[1280,1280]{1,0:T(8,128)} copy(f32[1280,1280]{0,1:T(8,128)} %convolution_bitcast_fusion) | data formatting | bytes 13107200
  137.3 12.1 %convolution_bitcast_fusion.1 = f32[1,1280,1024]{1,2,0:T(8,128)} fusion(bf16[1280,1280]{1,0:T(8,128)(2,1)} %all-gather.2.cloned.1.call-done, f32[1024,1280]{1,0:T(8,128)} %get-tuple-element.29, f32[1280]{0:T(1024)S(1)} %broadcast_in_dim.10, f32[1280]{0:T(1024)S(1)} %mul.178, f32[1280]{0:T(1024)S(1)} %copy-done.1, f32[1280]{0:T(1024)S(1)} %mul.156, ...), kind=kOutput, calls=%fused_computation.18 | convolution fusion | flops 3380346880 | bytes 13798400 | tf_op jit(solution)/shard_map/io,nos->nis/dot_general | solution.py:42
  149.4 11.9 %copy.16 = f32[1,1280,1024]{2,0,1:T(1,128)} copy(f32[1,1280,1024]{1,2,0:T(8,128)} %convolution_bitcast_fusion.1) | data formatting | bytes 10485760 | tf_op jit(solution)/shard_map/io,nos->nis/transpose | solution.py:42
  161.3 6.4 %all-to-all-start.1 = ((f32[1,1280,1024]{2,0,1:T(1,128)}), f32[1,1280,1024]{2,0,1:T(1,128)}, u32[]{:S(2)}, u32[]{:S(2)}) async-start(f32[1,1280,1024]{2,0,1:T(1,128)} %copy.16), calls=%async_computation.1 | async-start | bytes 10485760 | tf_op jit(solution)/shard_map/all_to_all | solution.py:45
  167.7 133.2 %reduce-scatter.4.cloned.1.call-done = f32[80,1280]{1,0:T(8,128)} async-done(((f32[1280,1280]{1,0:T(8,128)}), f32[80,1280]{1,0:T(8,128)}) %reduce-scatter.4.cloned.1.call-update) | async-done | bytes 409616
  300.9 2.1 copy.21
  303.1 55.1 %all-reduce = (f32[3,1280]{1,0:T(4,128)S(1)}, f32[]{:T(128)}) all-reduce(f32[3,1280]{1,0:T(4,128)S(1)} %pad_maximum_fusion, f32[]{:T(128)} %bitcast.9), channel_id=1, replica_groups=mesh['dp'=2,'mp'=16] {'mp'}, use_global_device_ids=true, to_apply=%region_15.16 | all-reduce | flops 3841 | bytes 30728 | tf_op jit(solution)/shard_map/psum | solution.py:11
  358.1 8.4 %all-reduce.1 = (f32[3,1280]{1,0:T(4,128)}, f32[]{:T(128)}) all-reduce(f32[3,1280]{1,0:T(4,128)S(1)} %get-tuple-element.24, f32[]{:T(128)} %get-tuple-element.25), channel_id=1, replica_groups=mesh['dp'=2,'mp'=16] {'dp'}, use_global_device_ids=true, to_apply=%region_16.17 | all-reduce | flops 3841 | bytes 30728 | tf_op jit(solution)/shard_map/psum | solution.py:12
  367.2 6.1 %copy.22 = f32[1,1280,1024]{2,1,0:T(8,128)} copy(f32[1,1280,1024]{2,0,1:T(1,128)} %all-to-all-done.1) | data formatting | bytes 10485760
  373.4 2.1 copy.17
  (30 shorter events, 0.7 us)
Async XLA Ops:
  7.2 83.9 %all-gather.2.cloned.1.call-start = ((), (), s32[]{:S(2)}) async-start(), calls=%async_computation.3 | async-start | bytes 3481600 | tf_op jit(solution)/shard_map/all_gather | solution.py:34
  7.9 83.1 %all-to-all-start = ((bf16[16,80,1024]{2,1,0:T(8,128)(2,1)}), bf16[16,80,1024]{2,1,0:T(8,128)(2,1)S(1)}, u32[]{:S(2)}, u32[]{:S(2)}) async-start(bf16[16,80,1024]{2,1,0:T(8,128)(2,1)} %param.6), calls=%async_computation | async-start | bytes 5242880 | tf_op jit(solution)/shard_map/all_to_all | solution.py:35
  14.2 286.7 %reduce-scatter.4.cloned.1.call-start = ((), (), s32[]{:S(2)}) async-start(), calls=%async_computation.5 | async-start | bytes 6963200
  98.3 3.9 %copy-start = (f32[1280]{0:T(1024)S(1)}, f32[1280]{0:T(1024)}, u32[]{:S(2)}) copy-start(f32[1280]{0:T(1024)} %param.9) | copy-start | bytes 15364
  98.3 3.9 %copy-start.1 = (f32[1280]{0:T(1024)S(1)}, f32[1280]{0:T(1024)}, u32[]{:S(2)}) copy-start(f32[1280]{0:T(1024)} %param.8) | copy-start | bytes 15364
  98.7 7.7 %copy-start.2 = (f32[1280]{0:T(1024)S(1)}, f32[1280]{0:T(1024)}, u32[]{:S(2)}) copy-start(f32[1280]{0:T(1024)} %param.10) | copy-start | bytes 15364
  161.3 205.9 %all-to-all-start.1 = ((f32[1,1280,1024]{2,0,1:T(1,128)}), f32[1,1280,1024]{2,0,1:T(1,128)}, u32[]{:S(2)}, u32[]{:S(2)}) async-start(f32[1,1280,1024]{2,0,1:T(1,128)} %copy.16), calls=%async_computation.1 | async-start | bytes 10485760 | tf_op jit(solution)/shard_map/all_to_all | solution.py:45
  167.7 205.7 %all-reduce.4.cloned.1.call-start = ((), (), s32[]{:S(2)}) async-start(), calls=%async_computation.4 | async-start | bytes 1310720 | tf_op jit(solution)/shard_map/psum | solution.py:49
Sparse Core Ops, SparseCore 0:
  10.3 75.0 all-gather.1
  137.4 163.3 reduce-scatter.3
  303.2 30.4 all-reduce.3
